TPU v7x, 32 devices: a whole 2x2x4 slice. The times are simulated.
32 devices in a mesh: dp: 16 (over z, y, core), local: 2 (over x).
Axes of the slice: x: 2, y: 2, z: 4, core: 2. Of those that a mesh axis runs over, the one named last changes fastest.
Arguments:
- pre_glu: bfloat16 [32, 256, 3072], P(('dp', 'local')), may hold values from -80 to 80
- lengths: int32 [32], P(('dp', 'local')), may hold values from 1 to 256, as said below
- kernel: float32 [5, 1536], replicated, may hold values from -2.5 to 2.5
- bn_gain: float32 [1536], replicated, may hold values from 0.5 to 2
- bn_shift: float32 [1536], replicated, may hold values from -1 to 1
- w_out: bfloat16 [1536, 1536], replicated, may hold values from -0.15625 to 0.15625
- cotangent: bfloat16 [32, 256, 1536], P(('dp', 'local')), may hold values from -6 to 6
Outputs:
- grad_pre_glu: bfloat16 [32, 256, 3072], P(('dp', 'local'))
- grad_w_out: float32 [1536, 1536], P('dp', 'local')
- grad_kernel: float32 [5, 1536], replicated
- grad_gain: float32 [1536], replicated
- grad_shift: float32 [1536], replicated
Inputs may be any that keep to these rules, and one draw needn't show every extreme that they name: `lengths`: each utterance's valid frames are its first ones; some utterance has all 256 frames valid.
All inputs are finite; a program needn't handle non-finite values.
Results may differ from a plain program's by a relative error of at most 0.0029.
Values sent between devices are 32-bit elements; how exact they have to be, the bound alone decides.
A program may use at most 64 MiB of HBM per device.

v0:
```python
import jax
import jax.numpy as jnp
from jax import lax
from jax.sharding import PartitionSpec as P

epsilon = 1e-05


def on_device(pre_glu, lengths, kernel, bn_gain, bn_shift, w_out, cotangent):
    frames = pre_glu.shape[1]
    model_width = kernel.shape[1]
    kernel_taps = kernel.shape[0]
    half_width = (kernel_taps - 1) // 2
    replicas = lax.axis_size("dp") * lax.axis_size("local")
    valid_mask = (jnp.arange(frames, dtype=jnp.int32)[:, None] < lengths[0]).astype(jnp.float32)
    first_half = pre_glu[0, :, :model_width].astype(jnp.float32)
    gate_value = jax.nn.sigmoid(pre_glu[0, :, model_width:].astype(jnp.float32))
    glu_out = first_half * gate_value * valid_mask
    padded = jnp.pad(glu_out, ((half_width, half_width), (0, 0)))
    conv_out = kernel[0] * padded[0:frames]
    for j in range(1, kernel_taps):
        conv_out = conv_out + kernel[j] * padded[j : j + frames]
    own_count = lengths[0].astype(jnp.float32)
    sum_first, sum_square, frame_total = lax.psum(
        (
            jnp.sum(conv_out * valid_mask, 0),
            jnp.sum(conv_out * conv_out * valid_mask, 0),
            own_count,
        ),
        ("dp", "local"),
    )
    mean_value = sum_first / frame_total
    variance = sum_square / frame_total - mean_value * mean_value
    invstd = lax.rsqrt(variance + epsilon)
    normed = (conv_out - mean_value) * invstd
    act_in = bn_gain * normed + bn_shift
    sig_act = jax.nn.sigmoid(act_in)
    swished = (act_in * sig_act).astype(jnp.bfloat16)
    masked_cot = cotangent[0] * valid_mask.astype(jnp.bfloat16)
    contract = (((0,), (0,)), ((), ()))
    wgrad_term = lax.dot_general(swished, masked_cot, contract, preferred_element_type=jnp.float32)
    partial_value = lax.psum_scatter(wgrad_term, "dp", scatter_dimension=0, tiled=True)
    weight_shard = lax.psum_scatter(partial_value, "local", scatter_dimension=1, tiled=True)
    grad_swish = lax.dot_general(
        masked_cot, w_out, (((1,), (1,)), ((), ())), preferred_element_type=jnp.float32
    )
    grad_act = grad_swish * sig_act * (1.0 + act_in * (1.0 - sig_act))
    channel_scale = bn_gain * invstd
    sum_shift, sum_gain = lax.psum(
        (jnp.sum(grad_act, 0), jnp.sum(grad_act * normed, 0)), ("dp", "local")
    )
    grad_conv = (
        valid_mask * channel_scale * (grad_act - (sum_shift + normed * sum_gain) / frame_total)
    )
    kernel_part = jnp.stack(
        [jnp.sum(grad_conv * padded[j : j + frames], 0) for j in range(kernel_taps)], 0
    )
    kernel_sum = lax.psum(kernel_part, ("dp", "local"))
    grad_padded = jnp.pad(grad_conv, ((half_width, half_width), (0, 0)))
    grad_glu = kernel[0] * grad_padded[kernel_taps - 1 : kernel_taps - 1 + frames]
    for j in range(1, kernel_taps):
        grad_glu = (
            grad_glu + kernel[j] * grad_padded[kernel_taps - 1 - j : kernel_taps - 1 - j + frames]
        )
    grad_glu = grad_glu * valid_mask
    grad_first = grad_glu * gate_value
    grad_second = grad_glu * first_half * gate_value * (1.0 - gate_value)
    grad_pre = jnp.concatenate([grad_first, grad_second], 1).astype(jnp.bfloat16)[None]
    return (
        grad_pre,
        weight_shard / replicas,
        kernel_sum / replicas,
        sum_gain / replicas,
        sum_shift / replicas,
    )


def solution(mesh):
    return jax.shard_map(
        on_device,
        mesh=mesh,
        in_specs=(
            P(("dp", "local"), None, None),
            P(("dp", "local")),
            P(),
            P(),
            P(),
            P(),
            P(("dp", "local"), None, None),
        ),
        out_specs=(P(("dp", "local"), None, None), P("dp", "local"), P(), P(), P()),
        check_vma=False,
    )
```

profile of v0, /device:TPU:0, one launch (start us, length us, event | category | flops | bytes accessed | tf_op | source)
XLA Modules:
  0.0 228.4 jit_solution(6184416316779539486)
XLA Ops:
  7.2 0.0 reduce-scatter.3.cloned.1.call-start
  7.9 1.1 slice_reduce_fusion.4
  9.0 1.8 fusion.1
  10.8 0.0 copy-start.2
  10.8 1.1 multiply_reduce_fusion.7
  11.9 42.4 %all-reduce.3 = (f32[1536]{0:T(1024)S(1)}, f32[]{:T(128)}, f32[1536]{0:T(1024)S(1)}) all-reduce(f32[1536]{0:T(1024)S(1)} %get-tuple-element.11, f32[]{:T(128)S(6)} %convert_element_type.50, f32[1536]{0:T(1024)S(1)} %get-tuple-element.10), channel_id=1, replica_groups=mesh['dp'=16,'local'=2] {'dp','local'}, use_global_device_ids=true, to_apply=%region_4.5 | all-reduce | flops 3073 | bytes 24584 | tf_op jit(solution)/shard_map/psum | solution.py:24
  54.4 0.7 fusion.17
  55.0 0.7 add_rsqrt_fusion
  55.7 6.4 %fusion.7 = f32[1536,1536]{1,0:T(8,128)} fusion(f32[256,1536]{1,0:T(8,128)S(1)} %get-tuple-element.29, f32[1536]{0:T(1024)S(1)} %copy-done.3, f32[1536]{0:T(1024)S(1)} %add_rsqrt_fusion, f32[1536]{0:T(1024)S(1)} %get-tuple-element.28, f32[1536]{0:T(1024)S(1)} %copy-done.2, bf16[1,256,1536]{2,1,0:T(8,128)(2,1)} %param.13, bf16[256]{0:T(256)(128)(2,1)S(1)} %fusion.18), kind=kOutput, calls=%fused_computation.33 | convolution fusion | flops 1211891712 | bytes 11821568 | tf_op jit(solution)/shard_map/dot_general | solution.py:41
  62.1 0.0 reduce-scatter.3.cloned.1.call-update
  62.2 0.0 reduce-scatter.5.cloned.1.call-start
  62.2 5.6 %fusion.20 = (f32[1536]{0:T(1024)S(1)}, f32[1536]{0:T(1024)S(1)}, f32[256,1536]{1,0:T(8,128)}) fusion(f32[1536]{0:T(1024)S(1)} %add_rsqrt_fusion, f32[256,1536]{1,0:T(8,128)S(1)} %get-tuple-element.29, f32[1536]{0:T(1024)S(1)} %get-tuple-element.28, f32[1536]{0:T(1024)S(1)} %copy-done.3, f32[1536]{0:T(1024)S(1)} %copy-done.2, ...), kind=kOutput, calls=%fused_computation.60 | convolution fusion | flops 1214247936 | bytes 8688128 | tf_op jit(solution)/shard_map/dot_general | solution.py:44
  67.8 41.1 %all-reduce.2 = (f32[1536]{0:T(1024)S(1)}, f32[1536]{0:T(1024)S(1)}) all-reduce(f32[1536]{0:T(1024)S(1)} %get-tuple-element.13, f32[1536]{0:T(1024)S(1)} %get-tuple-element.12), channel_id=1, replica_groups=mesh['dp'=16,'local'=2] {'dp','local'}, use_global_device_ids=true, to_apply=%region_8.9 | all-reduce | flops 3072 | bytes 24576 | tf_op jit(solution)/shard_map/psum | solution.py:49
  108.9 3.5 %multiply_reduce_fusion = (f32[1536]{0:T(1024)S(1)}, f32[1536]{0:T(1024)S(1)}, f32[1536]{0:T(1024)S(1)}, f32[1536]{0:T(1024)S(1)}, f32[1536]{0:T(1024)S(1)}, /*index=5*/f32[256,1536]{1,0:T(8,128)S(1)}) fusion(f32[256,1536]{1,0:T(8,128)S(1)} %fusion.1, f32[256,1536]{1,0:T(8,128)} %get-tuple-element.30, f32[]{:T(128)} %get-tuple-element.22, ...), kind=kLoop, calls=%fused_computation.12 | loop fusion | flops 7070208 | bytes 6353924 | tf_op jit(solution)/shard_map/reduce_sum | solution.py:56
  112.4 2.2 fusion.8
  114.6 59.1 %reduce-scatter.3.cloned.1.call-done = f32[96,1536]{1,0:T(8,128)} async-done(((f32[1536,1536]{1,0:T(8,128)}), f32[96,1536]{1,0:T(8,128)}) %reduce-scatter.3.cloned.1.call-update) | async-done | bytes 589840 | tf_op jit(solution)/shard_map/reduce_scatter | solution.py:42
  173.7 0.0 reduce-scatter.5.cloned.1.call-update
  173.7 1.4 fusion.9
  175.2 0.1 stack.23
  175.2 40.7 %psum.47 = f32[5,1536]{1,0:T(8,128)S(1)} all-reduce(f32[5,1536]{1,0:T(8,128)S(1)} %stack.23), channel_id=1, replica_groups=mesh['dp'=16,'local'=2] {'dp','local'}, use_global_device_ids=true, to_apply=%region_16.17 | all-reduce | flops 7680 | bytes 61440 | tf_op jit(solution)/shard_map/psum | solution.py:58
  216.0 0.6 broadcast_multiply_fusion.2
  216.6 2.7 %pad_maximum_fusion = bf16[1,256,3072]{2,1,0:T(8,128)(2,1)} fusion(bf16[1,256,1536]{2,1,0:T(8,128)(2,1)} %fusion.9, bf16[1,256,1536]{2,1,0:T(8,128)(2,1)} %get-tuple-element.25), kind=kLoop, calls=%fused_computation.8 | loop fusion | flops 3145728 | bytes 3145728 | tf_op jit(solution)/shard_map/concatenate | solution.py:68
  219.2 0.6 broadcast_multiply_fusion.1
  219.9 1.7 broadcast_multiply_fusion
  (15 shorter events, 0.1 us)
Async XLA Ops:
  7.2 166.5 %reduce-scatter.3.cloned.1.call-start = ((), (), s32[]{:S(2)}) async-start(), calls=%async_computation.2 | async-start | bytes 10027008 | tf_op jit(solution)/shard_map/reduce_scatter | solution.py:42
  10.8 43.6 %copy-start.2 = (f32[1536]{0:T(1024)S(1)}, f32[1536]{0:T(1024)}, u32[]{:S(2)}) copy-start(f32[1536]{0:T(1024)} %param.10) | copy-start | bytes 18436
  10.8 44.9 %copy-start.3 = (f32[1536]{0:T(1024)S(1)}, f32[1536]{0:T(1024)}, u32[]{:S(2)}) copy-start(f32[1536]{0:T(1024)} %param.11) | copy-start | bytes 18436
  62.2 157.7 %reduce-scatter.5.cloned.1.call-start = ((), (), s32[]{:S(2)}) async-start(), calls=%async_computation.3 | async-start | bytes 884736 | tf_op jit(solution)/shard_map/reduce_scatter | solution.py:43
  108.9 3.5 %copy-start = (bf16[1,256,3072]{2,1,0:T(8,128)(2,1)S(1)}, bf16[1,256,3072]{2,1,0:T(8,128)(2,1)}, u32[]{:S(2)}) copy-start(bf16[1,256,3072]{2,1,0:T(8,128)(2,1)} %param.7) | copy-start | bytes 4718596
  112.4 61.3 %copy-start.1 = (bf16[1,256,3072]{2,1,0:T(8,128)(2,1)S(1)}, bf16[1,256,3072]{2,1,0:T(8,128)(2,1)}, u32[]{:S(2)}) copy-start(bf16[1,256,3072]{2,1,0:T(8,128)(2,1)} %param.7) | copy-start | bytes 4718596
Sparse Core Ops, SparseCore 0:
  62.3 111.3 reduce-scatter.2
  175.9 15.2 reduce-scatter.4
where the time goes:
time: 229 us; the launch traced here: 228 us
  blocking collectives  124 us (54%)
  waiting for transfers between devices  59.1 us (26%)
  other arithmetic  16.9 us (7%)
  between operations  14.8 us (6%)
  matrix products  12 us (5%)
    reduce_scatter x1, waiting for transfers between devices, on_device(): lax.psum_scatter(wgrad_term, 'dp', scatter_dimension=0, tiled=True)  59.1 us
    psum x1, blocking collectives, on_device(): lax.psum((jnp.sum(conv_out * valid_mask, 0), jnp.sum(conv_out * conv_out...  42.4 us
    psum x1, blocking collectives, on_device(): lax.psum((jnp.sum(grad_act, 0), jnp.sum(grad_act * normed, 0)), ('dp', 'l...  41.1 us
    psum x1, blocking collectives, on_device(): kernel_sum = lax.psum(kernel_part, ('dp', 'local'))  40.7 us
    dot_general x1, matrix products, on_device(): lax.dot_general(swished, masked_cot, contract, preferred_element_type=jnp...  6.43 us
    concatenate x3, other arithmetic, on_device(): jnp.concatenate([grad_first, grad_second], 1).astype(jnp.bfloat16)[None]  6.24 us
    dot_general x1, matrix products, on_device(): lax.dot_general(masked_cot, w_out, (((1,), (1,)), ((), ())), preferred_el...  5.56 us
  transfers between devices with their start and end apart: 2, of which 1 were waited for; matrix products, arithmetic and copies ran while one was open for 7% of the time, Pallas kernels for 0%

commit v1 on v0

--- a/solution.py
+++ b/solution.py
@@ -55,7 +55,7 @@
     kernel_part = jnp.stack(
         [jnp.sum(grad_conv * padded[j : j + frames], 0) for j in range(kernel_taps)], 0
     )
-    kernel_sum = lax.psum(kernel_part, ("dp", "local"))
+    kernel_sum = jnp.sum(lax.all_gather(kernel_part, ("dp", "local")), axis=0)
     grad_padded = jnp.pad(grad_conv, ((half_width, half_width), (0, 0)))
     grad_glu = kernel[0] * grad_padded[kernel_taps - 1 : kernel_taps - 1 + frames]
     for j in range(1, kernel_taps):

time: 229 us -> 261 us (1.14)
  blocking collectives: 124 us -> 159 us
  waiting for transfers between devices: 59.1 us -> 54.4 us
    all_gather x0 -> x1, blocking collectives: none -> 75.7 us  [on_device(): kernel_sum = jnp.sum(lax.all_gather(kernel_part, ('dp', 'local')), axis=0)]
    psum x1 -> x0, blocking collectives: 40.7 us -> none  [on_device(): kernel_sum = lax.psum(kernel_part, ('dp', 'local'))]
    reduce_scatter x1, waiting for transfers between devices: 59.1 us -> 54.4 us  [on_device(): lax.psum_scatter(wgrad_term, 'dp', scatter_dimension=0, tiled=True)]
where the time goes in v1:
time: 261 us
  blocking collectives  159 us (61%)
  waiting for transfers between devices  54.4 us (21%)
  other arithmetic  18.9 us (7%)
  between operations  14.8 us (6%)
  matrix products  12 us (5%)
    all_gather x1, blocking collectives, on_device(): kernel_sum = jnp.sum(lax.all_gather(kernel_part, ('dp', 'local')), axis=0)  75.7 us
    reduce_scatter x1, waiting for transfers between devices, on_device(): lax.psum_scatter(wgrad_term, 'dp', scatter_dimension=0, tiled=True)  54.4 us
    psum x1, blocking collectives, on_device(): lax.psum((jnp.sum(conv_out * valid_mask, 0), jnp.sum(conv_out * conv_out...  42.4 us
    psum x1, blocking collectives, on_device(): lax.psum((jnp.sum(grad_act, 0), jnp.sum(grad_act * normed, 0)), ('dp', 'l...  41.1 us
    concatenate x3, other arithmetic, on_device(): jnp.concatenate([grad_first, grad_second], 1).astype(jnp.bfloat16)[None]  7.43 us
    dot_general x1, matrix products, on_device(): lax.dot_general(swished, masked_cot, contract, preferred_element_type=jnp...  6.43 us
    dot_general x1, matrix products, on_device(): lax.dot_general(masked_cot, w_out, (((1,), (1,)), ((), ())), preferred_el...  5.56 us
  transfers between devices with their start and end apart: 2, of which 1 were waited for; matrix products, arithmetic and copies ran while one was open for 7% of the time, Pallas kernels for 0%

profile of v1, /device:TPU:0, one launch (start us, length us, event | category | flops | bytes accessed | tf_op | source)
XLA Modules:
  0.0 260.6 jit_solution(2931396110375079881)
XLA Ops:
  7.2 0.0 reduce-scatter.3.cloned.1.call-start
  7.9 1.1 slice_reduce_fusion.4
  9.0 1.8 fusion.1
  10.8 1.1 multiply_reduce_fusion.7
  11.9 42.4 %all-reduce.3 = (f32[1536]{0:T(1024)S(1)}, f32[]{:T(128)}, f32[1536]{0:T(1024)S(1)}) all-reduce(f32[1536]{0:T(1024)S(1)} %get-tuple-element.11, f32[]{:T(128)S(6)} %convert_element_type.50, f32[1536]{0:T(1024)S(1)} %get-tuple-element.10), channel_id=1, replica_groups=mesh['dp'=16,'local'=2] {'dp','local'}, use_global_device_ids=true, to_apply=%region_4.5 | all-reduce | flops 3073 | bytes 24584 | tf_op jit(solution)/shard_map/psum | solution.py:24
  54.4 0.7 fusion.17
  55.0 0.7 add_rsqrt_fusion
  55.7 6.4 %fusion.7 = f32[1536,1536]{1,0:T(8,128)} fusion(f32[256,1536]{1,0:T(8,128)S(1)} %get-tuple-element.29, f32[1536]{0:T(1024)S(1)} %copy-done.2, f32[1536]{0:T(1024)S(1)} %add_rsqrt_fusion, f32[1536]{0:T(1024)S(1)} %get-tuple-element.28, f32[1536]{0:T(1024)S(1)} %copy-done.1, bf16[1,256,1536]{2,1,0:T(8,128)(2,1)} %param.13, bf16[256]{0:T(256)(128)(2,1)S(1)} %fusion.18), kind=kOutput, calls=%fused_computation.33 | convolution fusion | flops 1211891712 | bytes 11821568 | tf_op jit(solution)/shard_map/dot_general | solution.py:41
  62.1 0.0 reduce-scatter.3.cloned.1.call-update
  62.2 0.0 reduce-scatter.5.cloned.1.call-start
  62.2 5.6 %fusion.20 = (f32[1536]{0:T(1024)S(1)}, f32[1536]{0:T(1024)S(1)}, f32[256,1536]{1,0:T(8,128)}) fusion(f32[1536]{0:T(1024)S(1)} %add_rsqrt_fusion, f32[256,1536]{1,0:T(8,128)S(1)} %get-tuple-element.29, f32[1536]{0:T(1024)S(1)} %get-tuple-element.28, f32[1536]{0:T(1024)S(1)} %copy-done.2, f32[1536]{0:T(1024)S(1)} %copy-done.1, ...), kind=kOutput, calls=%fused_computation.60 | convolution fusion | flops 1214247936 | bytes 8688128 | tf_op jit(solution)/shard_map/dot_general | solution.py:44
  67.8 41.1 %all-reduce.2 = (f32[1536]{0:T(1024)S(1)}, f32[1536]{0:T(1024)S(1)}) all-reduce(f32[1536]{0:T(1024)S(1)} %get-tuple-element.13, f32[1536]{0:T(1024)S(1)} %get-tuple-element.12), channel_id=1, replica_groups=mesh['dp'=16,'local'=2] {'dp','local'}, use_global_device_ids=true, to_apply=%region_8.9 | all-reduce | flops 3072 | bytes 24576 | tf_op jit(solution)/shard_map/psum | solution.py:49
  108.9 4.2 %multiply_reduce_fusion = (f32[1536]{0:T(1024)S(1)}, f32[1536]{0:T(1024)S(1)}, f32[1536]{0:T(1024)S(1)}, f32[1536]{0:T(1024)S(1)}, f32[1536]{0:T(1024)S(1)}, /*index=5*/f32[256,1536]{1,0:T(8,128)}) fusion(f32[256,1536]{1,0:T(8,128)S(1)} %fusion.1, f32[256,1536]{1,0:T(8,128)} %get-tuple-element.30, f32[]{:T(128)} %get-tuple-element.22, ...), kind=kLoop, calls=%fused_computation.12 | loop fusion | flops 7070208 | bytes 6353924 | tf_op jit(solution)/shard_map/reduce_sum | solution.py:56
  113.1 0.1 stack.23
  113.2 5.5 %fusion.8 = (bf16[1,256,1536]{2,1,0:T(8,128)(2,1)S(1)}, f32[256,1536]{1,0:T(8,128)S(1)}) fusion(bf16[1,256,3072]{2,1,0:T(8,128)(2,1)} %param.7, f32[256]{0:T(256)S(1)} %compare_convert_fusion, f32[1536]{0:T(1024)S(1)} %get-tuple-element.17, f32[1536]{0:T(1024)S(1)} %get-tuple-element.18, f32[256,1536]{1,0:T(8,128)} %get-tuple-element.24, ...), kind=kLoop, calls=%fused_computation.34 | loop fusion | flops 6291456 | bytes 4750336 | tf_op jit(solution)/shard_map/concatenate | solution.py:68
  118.7 0.5 fusion.9
  119.3 54.4 %reduce-scatter.3.cloned.1.call-done = f32[96,1536]{1,0:T(8,128)} async-done(((f32[1536,1536]{1,0:T(8,128)}), f32[96,1536]{1,0:T(8,128)}) %reduce-scatter.3.cloned.1.call-update) | async-done | bytes 589840 | tf_op jit(solution)/shard_map/reduce_scatter | solution.py:42
  173.7 0.0 reduce-scatter.5.cloned.1.call-update
  173.7 75.7 %all-gather.1 = f32[32,5,1536]{2,1,0:T(8,128)S(1)} all-gather(f32[1,5,1536]{2,1,0:T(8,128)S(1)} %bitcast.33), channel_id=2, replica_groups=mesh['dp'=16,'local'=2] {'dp','local'}, dimensions={0}, use_global_device_ids=true | all-gather | bytes 1013760 | tf_op jit(solution)/shard_map/all_gather | solution.py:58
  249.4 0.1 reduce_sum.99
  249.5 0.6 broadcast_multiply_fusion.2
  250.1 1.4 pad_maximum_fusion
  251.5 0.6 broadcast_multiply_fusion.1
  252.1 1.7 broadcast_multiply_fusion
  (14 shorter events, 0.1 us)
Async XLA Ops:
  7.2 166.5 %reduce-scatter.3.cloned.1.call-start = ((), (), s32[]{:S(2)}) async-start(), calls=%async_computation.2 | async-start | bytes 10027008 | tf_op jit(solution)/shard_map/reduce_scatter | solution.py:42
  10.8 43.6 %copy-start.1 = (f32[1536]{0:T(1024)S(1)}, f32[1536]{0:T(1024)}, u32[]{:S(2)}) copy-start(f32[1536]{0:T(1024)} %param.10) | copy-start | bytes 18436
  10.8 44.9 %copy-start.2 = (f32[1536]{0:T(1024)S(1)}, f32[1536]{0:T(1024)}, u32[]{:S(2)}) copy-start(f32[1536]{0:T(1024)} %param.11) | copy-start | bytes 18436
  62.2 189.9 %reduce-scatter.5.cloned.1.call-start = ((), (), s32[]{:S(2)}) async-start(), calls=%async_computation.3 | async-start | bytes 884736 | tf_op jit(solution)/shard_map/reduce_scatter | solution.py:43
  113.2 5.5 %copy-start = (bf16[1,256,3072]{2,1,0:T(8,128)(2,1)S(1)}, bf16[1,256,3072]{2,1,0:T(8,128)(2,1)}, u32[]{:S(2)}) copy-start(bf16[1,256,3072]{2,1,0:T(8,128)(2,1)} %param.7) | copy-start | bytes 4718596
Sparse Core Ops, SparseCore 0:
  62.3 111.3 reduce-scatter.2
  175.9 18.5 reduce-scatter.4
